TPU v7x, 16 devices: a 4x2x1 block of a 4x4x8 slice. The times are simulated.
16 devices in a mesh: rep: 2 (over y, z), data: 8 (over x, core).
Axes of the slice: x: 4, y: 2, z: 1, core: 2. Of those that a mesh axis runs over, the one named last changes fastest.
The devices are a block of a 4x4x8 slice.
Arguments:
- x: bfloat16 [1024, 1536], P(('rep', 'data')), parts along dimension 0
- adapter_id: int32 [1024], P(('rep', 'data')), parts along dimension 0
- w_gate: bfloat16 [1536, 8960], replicated
- w_up: bfloat16 [1536, 8960], replicated
- w_down: bfloat16 [8960, 1536], replicated
- a_gate: bfloat16 [1024, 8, 1536], P('data')
- b_gate: bfloat16 [1024, 8, 8960], P('data')
- a_up: bfloat16 [1024, 8, 1536], P('data')
- b_up: bfloat16 [1024, 8, 8960], P('data')
- a_down: bfloat16 [1024, 8, 8960], P('data')
- b_down: bfloat16 [1024, 8, 1536], P('data')
Outputs:
- output: bfloat16 [1024, 1536], P(('rep', 'data')), parts along dimension 0
There are 2 independent parts. A program takes and returns all parts, laid end to end along the dimension named above; an argument that names none is the same for every part.
All inputs are finite; a program needn't handle non-finite values.
Results may differ from a plain program's by a relative error of at most 0.00571002.
Values are sent between devices in bfloat16 or wider.
A program may use at most 768 MiB of HBM per device.

v0:
```python
import functools

import jax
import jax.numpy as jnp
from jax import lax
from jax.experimental import pallas as pl
from jax.experimental.pallas import tpu as pltpu
from jax.sharding import PartitionSpec as P

ALPHA = 32
SUB = 256
STEP_SUBS = 5
RING = 3
GROUPS = ((0, 3), (3, 2))
BF = jnp.bfloat16
F32 = jnp.float32


def nn(a, b):
    return jnp.dot(a, b, preferred_element_type=F32)


def nt(a, b):
    return lax.dot_general(a, b, (((1,), (1,)), ((), ())), preferred_element_type=F32)


def count_ge(v, width, groups):
    total = jnp.zeros(v.shape, jnp.int32)
    for g in range(1, groups):
        total += (v >= g * width).astype(jnp.int32)
    return total


def layer_kernel(groups, rank, cap, per_owner, x_hbm, ids_hbm, wg, wu, wd, ag, au, bg, bu, ad, bd, out_ref,
                 send, recv, rows, low_g, low_u, hid, low_d, ret, got, b_buf, ad_t, big, all_ids, first, x_ref, ids_ref,
                 ring_sem, a_sem, b_sem, wd_sem, out_sem, in_sem, rs_sem, rr_sem, x_sem, id_out, id_in):
    toks, width = x_hbm.shape
    ff = wg.shape[1]
    ranks = per_owner * rank
    slots = groups * cap
    scale = ALPHA / rank
    step = STEP_SUBS * SUB
    n_steps = ff // step
    ring_rows = 2 * width + 3 * ranks
    fold = ff // STEP_SUBS
    cols = width // SUB
    whole = ((wg, 0, width), (wu, width, width), (bg, 2 * width, ranks), (bu, 2 * width + ranks, ranks), (ad, 2 * width + 2 * ranks, ranks))
    me = lax.axis_index("data")
    peers = [lax.rem(me + k, groups) for k in (4, 3, 5, 2, 6, 1, 7) if k < groups]

    def start_ring(c, which):
        slot = lax.rem(c, RING)
        for k, (lo, subs) in enumerate(GROUPS):
            col = pl.multiple_of(c * step + lo * SUB, 128)
            for i in which:
                src, off, n = whole[i]
                at = pl.multiple_of(slot * ring_rows + off, 8)
                pltpu.make_async_copy(src.at[:, pl.ds(col, subs * SUB)], big.at[pl.ds(at, n), pl.ds(lo * SUB, subs * SUB)], ring_sem.at[slot, k]).start()

    def landing(dst, sem):
        return pltpu.make_async_copy(dst, dst, sem)

    def ring_wait(c, k):
        slot = lax.rem(c, RING)
        lo, subs = GROUPS[k]
        landing(big.at[pl.ds(pl.multiple_of(slot * ring_rows, 8), ring_rows), pl.ds(lo * SUB, subs * SUB)], ring_sem.at[slot, k]).wait()

    def wd_at(j):
        return pl.multiple_of(ring_rows * (1 + j // 3) + lax.rem(j, 3) * fold, 8)

    def wd_copy(j, q):
        col = pl.multiple_of(j * SUB, 128)
        return pltpu.make_async_copy(wd.at[pl.ds(q * fold, fold), pl.ds(col, SUB)], big.at[pl.ds(wd_at(j), fold), pl.ds(q * SUB, SUB)], wd_sem.at[j])

    def start_wd(j):
        for q in range(STEP_SUBS):
            wd_copy(j, q).start()

    rest = width - step
    x_copies = [pltpu.make_async_copy(ids_hbm, ids_ref, x_sem.at[0]), pltpu.make_async_copy(x_hbm, x_ref, x_sem.at[1])]
    for cp in x_copies:
        cp.start()
    barrier = pltpu.get_barrier_semaphore()
    for p in peers:
        pl.semaphore_signal(barrier, inc=1, device_id={"data": p}, device_id_type=pl.DeviceIdType.MESH)

    t_base = (RING - 1) * ring_rows
    a_base = t_base + 2 * width
    a_copies = []
    for i, src in enumerate((ag, au)):
        a_copies.append(pltpu.make_async_copy(src.at[:, :step], big.at[pl.ds(a_base + i * ranks, ranks), :], a_sem.at[i]))
        a_copies.append(pltpu.make_async_copy(src.at[:, step:], big.at[pl.ds(a_base + 2 * ranks, ranks), pl.ds(i * rest, rest)], a_sem.at[i]))
    b_copy = pltpu.make_async_copy(bd, b_buf, b_sem)
    for cp in a_copies:
        cp.start()
    for c in range(2):
        start_ring(c, range(len(whole)))
    b_copy.start()

    for cp in x_copies:
        cp.wait()
    id_row = ids_ref[...]
    sub_i = lax.broadcasted_iota(jnp.int32, (toks, toks), 0)
    lane_i = lax.broadcasted_iota(jnp.int32, (toks, toks), 1)
    id_col = jnp.sum(jnp.where(sub_i == lane_i, jnp.broadcast_to(id_row, (toks, toks)), 0), axis=1, keepdims=True)
    own_row = count_ge(id_row, per_owner, groups)
    own_col = count_ge(id_col, per_owner, groups)
    same = own_col == own_row
    arr_col = jnp.sum((same & (lane_i < sub_i)).astype(jnp.int32), axis=1, keepdims=True)
    arr_row = jnp.sum((same & (sub_i < lane_i)).astype(jnp.int32), axis=0, keepdims=True)
    to_slot = (lax.broadcasted_iota(jnp.int32, (slots, toks), 0) == own_row * cap + arr_row).astype(F32).astype(BF)
    send[...] = nn(to_slot, x_ref[...]).reshape(groups, cap, width).astype(BF)

    with jax.named_scope('entry_wait'):
        pl.semaphore_wait(barrier, groups - 1)

    def row_copy(p):
        return pltpu.make_async_remote_copy(src_ref=send.at[p], dst_ref=recv.at[me], send_sem=out_sem, recv_sem=in_sem,
                                            device_id={"data": p}, device_id_type=pl.DeviceIdType.MESH)

    def id_copy(p, at):
        return pltpu.make_async_remote_copy(src_ref=ids_ref, dst_ref=all_ids.at[at], send_sem=id_out, recv_sem=id_in.at[at],
                                            device_id={"data": p}, device_id_type=pl.DeviceIdType.MESH)

    for p in peers:
        id_copy(p, me).start()
    for p in peers:
        row_copy(p).start()
    all_ids[me] = ids_ref[...]
    recv[me] = send[me]
    for i in range(2):
        landing(b_buf, a_sem.at[i]).wait()
    for i in range(2):
        for r in range(0, ranks, 128):
            turned = pl.ds(r, 128)
            big[t_base + i * width:t_base + i * width + step, turned] = big[a_base + i * ranks + r:a_base + i * ranks + r + 128, :].T
            big[t_base + i * width + step:t_base + (i + 1) * width, turned] = big[a_base + 2 * ranks + r:a_base + 2 * ranks + r + 128, i * rest:(i + 1) * rest].T
    start_ring(RING - 1, range(2, len(whole)))
    for p in peers:
        id_copy(p, p).wait_recv()
    every = jnp.concatenate([all_ids[g] for g in range(groups)], axis=0)
    every = every - me * per_owner
    mine = ((every >= 0) & (every < per_owner)).astype(F32)
    before = nn(mine.astype(BF), (sub_i < lane_i).astype(F32).astype(BF))
    slot_i = lax.broadcasted_iota(jnp.int32, (cap, toks), 0).astype(F32)
    value = mine * (every * rank).astype(F32)
    first[...] = jnp.concatenate([jnp.sum(jnp.where(slot_i == before[g:g + 1, :], value[g:g + 1, :], 0.0), axis=1, keepdims=True) for g in range(groups)], axis=0).astype(jnp.int32)

    def own():
        rank_i = lax.broadcasted_iota(jnp.int32, (slots, ranks), 1)
        return (rank_i >= first[...]) & (rank_i < first[...] + rank)

    with jax.named_scope('row_wait'):
        landing(recv.at[:groups - 1], in_sem).wait()

    rows[...] = recv[...].astype(F32).reshape(slots, width).astype(BF)
    lows = [nn(rows[...], big[t_base + i * width:t_base + (i + 1) * width, :ranks]) for i in range(2)]
    low_g[...] = jnp.where(own(), lows[0], 0.0).astype(BF)
    low_u[...] = jnp.where(own(), lows[1], 0.0).astype(BF)
    start_ring(RING - 1, range(2))
    low_d[...] = jnp.zeros_like(low_d)

    def half(base, col, w_off, w_n, b_off, low):
        full = nn(low[...], big[pl.ds(base + b_off, ranks), col])
        return nn(rows[...], big[pl.ds(base + w_off, w_n), col]) + (scale * full).astype(BF).astype(F32)

    def ff_step(c, carry):
        base = pl.multiple_of(lax.rem(c, RING) * ring_rows, 8)
        for k, (lo, subs) in enumerate(GROUPS):
            with jax.named_scope('ring_wait'):
                ring_wait(c, k)
            for s in range(lo, lo + subs):
                col = pl.ds(s * SUB, SUB)
                ad_t[s * SUB:(s + 1) * SUB, :] = big[pl.ds(base + 2 * width + 2 * ranks, ranks), col].T
                g = half(base, col, 0, width, 2 * width, low_g)
                u = half(base, col, width, width, 2 * width + ranks, low_u)
                hid[c * STEP_SUBS + s] = (g * jax.nn.sigmoid(g) * u).astype(BF)
        h = jnp.concatenate([hid[c * STEP_SUBS + s] for s in range(STEP_SUBS)], axis=1)
        low_d[...] += nn(h, ad_t[...])

        @pl.when(c + RING < n_steps)
        def _():
            start_ring(c + RING, range(len(whole)))

        for back in (0, 1):
            @pl.when(c == n_steps - 3 + back)
            def _(back=back):
                for j in range(3 * back, 3 * back + 3):
                    start_wd(j)

        return carry

    lax.fori_loop(0, n_steps, ff_step, 0)

    low_dm = jnp.where(own(), low_d[...], 0.0).astype(BF)
    low_g[...] = low_dm
    b_copy.wait()

    def back_copy(j, n, p):
        return pltpu.make_async_remote_copy(src_ref=ret.at[pl.ds(j, n), p], dst_ref=got.at[pl.ds(j, n), me], send_sem=rs_sem, recv_sem=rr_sem.at[j],
                                            device_id={"data": p}, device_id_type=pl.DeviceIdType.MESH)

    def columns(j, n):
        with jax.named_scope('wd_wait'):
            for k in range(n):
                landing(big.at[pl.ds(wd_at(j + k), fold), :], wd_sem.at[j + k]).wait()
        col = pl.ds(pl.multiple_of(j * SUB, 128), n * SUB)
        full = nn(low_g[...], b_buf[:, col])
        h = jnp.concatenate([hid[s] for s in range(ff // SUB)], axis=1)
        w = jnp.concatenate([jnp.concatenate([big[pl.ds(wd_at(j + k), fold), pl.ds(q * SUB, SUB)] for q in range(STEP_SUBS)], axis=0) for k in range(n)], axis=1)
        done = rows[:, col].astype(F32) + (nn(h, w) + (scale * full).astype(BF).astype(F32))
        for k in range(n):
            ret[j + k] = done[:, k * SUB:(k + 1) * SUB].reshape(groups, cap, SUB).astype(BF)
        for p in peers:
            back_copy(j, n, p).start()
        for k in range(n):
            got[j + k, me] = ret[j + k, me]

    def col_step(j, carry):
        columns(j, 1)
        return carry

    lax.fori_loop(0, cols, col_step, 0)

    to_tok = (lax.broadcasted_iota(jnp.int32, (toks, slots), 1) == own_col * cap + arr_col).astype(F32).astype(BF)
    for j, n in [(j, 1) for j in range(cols)]:
        with jax.named_scope('back_wait'):
            landing(got.at[pl.ds(j, n), :groups - 1], rr_sem.at[j]).wait()
        for k in range(j, j + n):
            block = got[k].astype(F32).reshape(slots, SUB).astype(BF)
            out_ref[:, k * SUB:(k + 1) * SUB] = nn(to_tok, block).astype(BF)
    with jax.named_scope('send_wait'):
        for p in peers:
            id_copy(p, p).wait_send()
        landing(send.at[:groups - 1], out_sem).wait()
        landing(ret.at[:, :groups - 1], rs_sem).wait()


def solution(mesh):
    groups = mesh.shape["data"]
    row_spec = P(("rep", "data"), None)
    id_spec = P(("rep", "data"))
    owned_spec = P("data", None, None)

    def device_step(x, adapter_id, w_gate, w_up, w_down, a_gate, b_gate, a_up, b_up, a_down, b_down):
        toks, width = x.shape
        per_owner, rank, ff = b_gate.shape
        ranks = per_owner * rank
        cap = (3 * toks + groups - 1) // groups
        slots = groups * cap
        cols = width // SUB
        ring_rows = 2 * width + 3 * ranks

        def flat(m):
            return m.reshape(ranks, m.shape[-1])

        return pl.pallas_call(
            functools.partial(layer_kernel, groups, rank, cap, per_owner),
            out_shape=pltpu.VMEM((toks, width), BF),
            in_specs=[pl.BlockSpec(memory_space=pl.ANY)] * 11,
            out_specs=pl.BlockSpec(memory_space=pltpu.VMEM),
            scratch_shapes=[
                pltpu.VMEM((groups, cap, width), BF),
                pltpu.VMEM((groups, cap, width), BF),
                pltpu.VMEM((slots, width), BF),
                pltpu.VMEM((slots, ranks), BF),
                pltpu.VMEM((slots, ranks), BF),
                pltpu.VMEM((ff // SUB, slots, SUB), BF),
                pltpu.VMEM((slots, ranks), F32),
                pltpu.VMEM((cols, groups, cap, SUB), BF),
                pltpu.VMEM((cols, groups, cap, SUB), BF),
                pltpu.VMEM((ranks, width), BF),
                pltpu.VMEM((STEP_SUBS * SUB, ranks), BF),
                pltpu.VMEM((RING * ring_rows, STEP_SUBS * SUB), BF),
                pltpu.VMEM((groups, 1, toks), jnp.int32),
                pltpu.VMEM((slots, 1), jnp.int32),
                pltpu.VMEM((toks, width), BF),
                pltpu.VMEM((1, toks), jnp.int32),
                pltpu.SemaphoreType.DMA((RING, len(GROUPS))),
                pltpu.SemaphoreType.DMA((2,)),
                pltpu.SemaphoreType.DMA,
                pltpu.SemaphoreType.DMA((cols,)),
                pltpu.SemaphoreType.DMA,
                pltpu.SemaphoreType.DMA,
                pltpu.SemaphoreType.DMA,
                pltpu.SemaphoreType.DMA((cols,)),
                pltpu.SemaphoreType.DMA((2,)),
                pltpu.SemaphoreType.DMA,
                pltpu.SemaphoreType.DMA((groups,)),
            ],
            compiler_params=pltpu.CompilerParams(collective_id=0, has_side_effects=True, vmem_limit_bytes=66_400_000),
            name="lora_layer",
        )(x, adapter_id.reshape(1, toks), w_gate, w_up, w_down, flat(a_gate), flat(a_up), flat(b_gate), flat(b_up), flat(a_down), flat(b_down))

    return jax.shard_map(device_step, mesh=mesh, in_specs=(row_spec, id_spec, P(), P(), P(), owned_spec, owned_spec, owned_spec, owned_spec, owned_spec, owned_spec), out_specs=row_spec, check_vma=False)
```

profile of v0, /device:TPU:113, one launch (start us, length us, event | category | flops | bytes accessed | tf_op | source)
XLA Modules:
  0.0 52.9 jit_solution(6875999226094232288)
XLA Ops:
  0.0 52.2 %lora_layer.1 = bf16[64,1536]{1,0:T(8,128)(2,1)S(1)} custom-call(bf16[64,1536]{1,0:T(8,128)(2,1)} %x_hbm.1, s32[1,64]{1,0:T(1,128)} %bitcast.13, bf16[1536,8960]{1,0:T(8,128)(2,1)} %wg.1, bf16[1536,8960]{1,0:T(8,128)(2,1)} %wu.1, bf16[8960,1536]{1,0:T(8,128)(2,1)} %wd.1, bf16[1024,1536]{1,0:T(8,128)(2,1)} %bitcast.10, bf16[1024,1536]{1,0:T(8,128)(2,1)} %bitcast.11, ...), custom_call_target="tpu_custom_call" | custom-call | tf_op jit(solution)/shard_map/lora_layer/pallas_call | solution.py:257
  52.2 0.7 %copy.13 = bf16[64,1536]{1,0:T(8,128)(2,1)} copy(bf16[64,1536]{1,0:T(8,128)(2,1)S(1)} %lora_layer.1) | data formatting | bytes 393216
where the time goes:
time: 52.9 us
  Pallas kernels  52.2 us (99%)
  local copies, waits for them, and re-layouts  0.68 us (1%)
    pallas_call x1, Pallas kernels, device_step(): pl.pallas_call(functools.partial(layer_kernel, groups, rank, cap, per_own...  52.2 us

commit v1 on v0

--- a/solution.py
+++ b/solution.py
@@ -95,7 +95,6 @@
         cp.start()
     for c in range(2):
         start_ring(c, range(len(whole)))
-    b_copy.start()
 
     for cp in x_copies:
         cp.wait()
@@ -185,6 +184,8 @@
         for back in (0, 1):
             @pl.when(c == n_steps - 3 + back)
             def _(back=back):
+                if back == 0:
+                    b_copy.start()
                 for j in range(3 * back, 3 * back + 3):
                     start_wd(j)
 

time: 52.9 us -> 55.2 us (1.043)
  Pallas kernels: 52.2 us -> 54.4 us
    pallas_call x1, Pallas kernels: 52.2 us -> 54.4 us  [device_step(): pl.pallas_call(functools.partial(layer_kernel, groups, rank, cap, per_own...]
where the time goes in v1:
time: 55.2 us; the launch traced here: 55.1 us
  Pallas kernels  54.4 us (99%)
  local copies, waits for them, and re-layouts  0.68 us (1%)
    pallas_call x1, Pallas kernels, device_step(): pl.pallas_call(functools.partial(layer_kernel, groups, rank, cap, per_own...  54.4 us

profile of v1, /device:TPU:113, one launch (start us, length us, event | category | flops | bytes accessed | tf_op | source)
XLA Modules:
  0.0 55.1 jit_solution(2415102486835922827)
XLA Ops:
  0.0 54.4 %lora_layer.1 = bf16[64,1536]{1,0:T(8,128)(2,1)S(1)} custom-call(bf16[64,1536]{1,0:T(8,128)(2,1)} %x_hbm.1, s32[1,64]{1,0:T(1,128)} %bitcast.13, bf16[1536,8960]{1,0:T(8,128)(2,1)} %wg.1, bf16[1536,8960]{1,0:T(8,128)(2,1)} %wu.1, bf16[8960,1536]{1,0:T(8,128)(2,1)} %wd.1, bf16[1024,1536]{1,0:T(8,128)(2,1)} %bitcast.10, bf16[1024,1536]{1,0:T(8,128)(2,1)} %bitcast.11, ...), custom_call_target="tpu_custom_call" | custom-call | tf_op jit(solution)/shard_map/lora_layer/pallas_call | solution.py:258
  54.4 0.7 %copy.13 = bf16[64,1536]{1,0:T(8,128)(2,1)} copy(bf16[64,1536]{1,0:T(8,128)(2,1)S(1)} %lora_layer.1) | data formatting | bytes 393216
